TPU v7x, 32 devices: a 4x4x1 block of a 4x4x8 slice. The times are simulated.
32 devices in a mesh: dp: 1 (over z), tp: 4 (over y), ep: 8 (over x, core).
Axes of the slice: x: 4, y: 4, z: 1, core: 2. Of those that a mesh axis runs over, the one named last changes fastest.
The devices are a block of a 4x4x8 slice.
Arguments:
- hidden_in: bfloat16 [1024, 2048], P(('dp', 'ep'))
- topk_idx: int32 [1024, 6], P(('dp', 'ep'))
- norm_gain: bfloat16 [2048], replicated
- router_w: bfloat16 [2048, 64], replicated
- shared_sig_w: bfloat16 [2048, 1], replicated
- exp_gate: bfloat16 [64, 2048, 1408], P('ep', None, 'tp')
- exp_up: bfloat16 [64, 2048, 1408], P('ep', None, 'tp')
- exp_down: bfloat16 [64, 1408, 2048], P('ep', 'tp')
- sh_gate: bfloat16 [2048, 2816], P(None, ('tp', 'ep'))
- sh_up: bfloat16 [2048, 2816], P(None, ('tp', 'ep'))
- sh_down: bfloat16 [2816, 2048], P(('tp', 'ep'))
Outputs:
- output: bfloat16 [1024, 2048], P(('dp', 'ep'))
All inputs are finite; a program needn't handle non-finite values.
Results may differ from a plain program's by a relative error of at most 0.0123824.
Values are sent between devices in bfloat16 or wider.
A program may use at most 768 MiB of HBM per device.

v0:
```python
import functools

import jax
import jax.numpy as jnp
from jax import lax
from jax.experimental import pallas as pl
from jax.experimental.pallas import tpu as pltpu
from jax.sharding import PartitionSpec as P

RMS_EPS = 1e-6
LANES = 128
PITCH = 20
PAD = 4
TILES = (64, 256, 320, 384, 512)
SLOTS = 3
F32 = jnp.float32
BF16 = jnp.bfloat16
NT = (((1,), (1,)), ((), ()))
TN = (((0,), (0,)), ((), ()))
MESH = pl.DeviceIdType.MESH


def place():
    ep, y = lax.axis_index("ep"), lax.axis_index("tp")
    return ep // 2, ep % 2, y, lax.axis_size("ep") // 2, lax.axis_size("tp")


def peer(x, core, y):
    return {"ep": 2 * x + core, "tp": y}


def remote(src, dst, send, recv, where):
    return pltpu.make_async_remote_copy(src_ref=src, dst_ref=dst, send_sem=send, recv_sem=recv,
                                        device_id=where, device_id_type=MESH)


def meet(peers):
    barrier = pltpu.get_barrier_semaphore()
    for p in peers:
        pl.semaphore_signal(barrier, inc=1, device_id=p, device_id_type=MESH)
    pl.semaphore_wait(barrier, len(peers))


def token_pair(x, gain, sigw, cols_ref, n_exp, width, up_at):
    xf = x.astype(F32)
    inv = lax.rsqrt(jnp.mean(xf * xf, axis=-1, keepdims=True) + RMS_EPS)
    h = (xf * inv * gain.astype(F32)).astype(BF16)
    sig = jax.nn.sigmoid(jnp.sum(h.astype(F32) * sigw.astype(F32), axis=-1, keepdims=True))
    return h, sig


def pair_dots(h, cols_ref, n_exp, width, up_at):
    out = lax.dot_general(cols_ref[...], h, NT, preferred_element_type=F32)
    logits = out[:n_exp]
    ex = jnp.exp(logits - jnp.max(logits, axis=0, keepdims=True))
    prob = ex / jnp.sum(ex, axis=0, keepdims=True)
    act = (jax.nn.silu(out[n_exp:n_exp + width]) * out[up_at:up_at + width]).astype(BF16)
    return prob, act


def routing_lists(idx_t, first, n_local, lst_ref, cnt_ref):
    n_tok = idx_t.shape[1]
    n_hi = n_tok // LANES
    sub = lax.broadcasted_iota(jnp.int32, (n_local, n_tok), 0)
    member = jnp.zeros((n_local, n_tok), F32)
    for e in range(n_local):
        hit = jnp.sum((idx_t == first + e).astype(F32), axis=0, keepdims=True)
        member = jnp.where(sub == e, hit, member)
    tri = (lax.broadcasted_iota(jnp.int32, (LANES, LANES), 0)
           < lax.broadcasted_iota(jnp.int32, (LANES, LANES), 1)).astype(F32).astype(BF16)
    base = jnp.zeros((n_local, 1), F32)
    parts = []
    for b in range(n_hi):
        m_b = member[:, b * LANES:(b + 1) * LANES]
        parts.append(jnp.dot(m_b.astype(BF16), tri, preferred_element_type=F32) + base)
        base = base + jnp.sum(m_b, axis=-1, keepdims=True)
    pos = jnp.concatenate(parts, axis=1).astype(jnp.int32)
    cnt_ref[...] = jnp.broadcast_to(base, cnt_ref.shape).astype(jnp.int32)
    tok = lax.broadcasted_iota(jnp.int32, (n_hi, n_tok), 1)
    hi_id = lax.broadcasted_iota(jnp.int32, (n_hi, n_tok), 0)
    lo_id = lax.broadcasted_iota(jnp.int32, (LANES, n_tok), 0)
    row_id = (lax.broadcasted_iota(jnp.int32, (n_hi, LANES), 0) * LANES
              + lax.broadcasted_iota(jnp.int32, (n_hi, LANES), 1))
    tok_hi = (tok >> 3).astype(F32)
    tok_lo = (tok & 7).astype(F32)
    for e in range(n_local):
        p_e = pos[e:e + 1, :]
        here = ((p_e >> 7) == hi_id) & (member[e:e + 1, :] > 0.0)
        lo_hot = jnp.where((p_e & (LANES - 1)) == lo_id, 1.0, 0.0).astype(BF16)
        lhs = jnp.concatenate([jnp.where(here, v, 0.0) for v in (tok_hi, tok_lo)], axis=0).astype(BF16)
        got = lax.dot_general(lhs, lo_hot, NT, preferred_element_type=F32)
        t_of = (got[:n_hi] * 8.0 + got[n_hi:]).astype(jnp.int32)
        valid = row_id < base[e:e + 1, :].astype(jnp.int32)
        lst_ref[e * n_hi:(e + 1) * n_hi, :] = jnp.where(valid, t_of, n_tok)


def gather_kernel(n_local, x_hbm, idx_hbm, gain_hbm, rw_hbm, sigw_hbm, shg_hbm, shu_hbm,
                  h_hbm, act_ref, sigv_ref, lst_ref, wl_ref, cnt_ref,
                  tok, idx, cols, gain_ref, sigw_ref, prob, hbuf, in_sem, send, recv, isend, irecv, out_sem):
    x, core, y, n_x, n_y = place()
    n_exp, width = rw_hbm.shape[0], shg_hbm.shape[0]
    up_at = n_exp + (width + 15) // 16 * 16
    rows = x_hbm.shape[0]
    half, piece = rows // 2, rows // 4
    own = 2 * x + core
    load_x = pltpu.make_async_copy(x_hbm, tok.at[own], in_sem.at[0])
    load_i = pltpu.make_async_copy(idx_hbm, idx.at[own], in_sem.at[1])
    load_x.start()
    load_i.start()
    small = [pltpu.make_async_copy(src, dst, in_sem.at[2 + k]) for k, (src, dst) in enumerate((
        (rw_hbm, cols.at[0:n_exp, :]), (shg_hbm, cols.at[n_exp:n_exp + width, :]),
        (shu_hbm, cols.at[up_at:up_at + width, :]), (gain_hbm, gain_ref), (sigw_hbm, sigw_ref)))]

    def at(v, n):
        return lax.rem(v + n, n)

    right, left, far = at(x + 1, n_x), at(x - 1, n_x), at(x + 2, n_x)
    up, down = at(y + 1, n_y), at(y - 1, n_y)
    meet([peer(x, 1 - core, y), peer(right, core, y), peer(left, core, y), peer(x, core, up), peer(x, core, down)])
    load_x.wait()
    load_i.wait()

    started = []
    count = [0]

    def copy(block, row, n_rows, where):
        k = count[0]
        count[0] += 1
        row = pl.multiple_of(row, piece)
        ref = tok.at[block, pl.ds(row, n_rows), :]
        c = remote(ref, ref, send.at[k], recv.at[k], where)
        return c

    def go(c):
        c.start()
        started.append(c)
        return c

    mine = (y % 2) * half
    m = [mine, mine + piece]
    o = [half - mine, half - mine + piece]
    to_right, to_left = peer(right, core, y), peer(left, core, y)
    to_up, to_down, to_mate = peer(x, core, up), peer(x, core, down), peer(x, 1 - core, y)
    icopies = []

    def send_idx(block, where):
        k = len(icopies)
        c = remote(idx.at[block], idx.at[block], isend.at[k], irecv.at[k], where)
        c.start()
        icopies.append(c)
        return c

    i_left, i_right, i_own = send_idx(own, to_right), send_idx(own, to_left), send_idx(own, to_mate)
    from_left, from_right = {}, {}
    for k in range(2):
        from_left[k] = go(copy(own, m[k], piece, to_right))
        from_right[1 - k] = go(copy(own, m[1 - k], piece, to_left))
    s_mate = go(copy(own, 0, rows, to_mate))

    cols[n_exp + width - width % 8:up_at, :] = jnp.zeros((up_at - n_exp - width + width % 8, cols.shape[1]), BF16)
    tail = up_at + width - width % 8
    cols[tail:, :] = jnp.zeros((cols.shape[0] - tail, cols.shape[1]), BF16)
    for c in small:
        c.start()

    outs = []

    def pair(slot, px):
        for c in range(2):
            h, sig = token_pair(tok[2 * px + c], gain_ref[...].astype(F32).reshape(1, -1), sigw_ref[...], cols, n_exp, width, up_at)
            hbuf[slot, c * rows:(c + 1) * rows, :] = h
            sigv_ref[pl.ds(pl.multiple_of((2 * px + c) * rows, rows), rows), :] = sig
        out = pltpu.make_async_copy(hbuf.at[slot], h_hbm.at[pl.ds(pl.multiple_of(2 * px * rows, 2 * rows), 2 * rows), :],
                                    out_sem.at[slot])
        p, a = pair_dots(hbuf[slot], cols, n_exp, width, up_at)
        prob[px] = p
        act_ref[:, pl.ds(pl.multiple_of(px * 2 * rows, 2 * rows), 2 * rows)] = a
        out.start()
        outs.append(out)

    lb, rb, fb = 2 * left + core, 2 * right + core, 2 * far + core
    mate = {name: [] for name in "lrf"}
    along_y, forward = {}, {}

    def relay(name, block, k, arrived, onward=None):
        arrived.wait_recv()
        if onward is not None:
            forward[k] = go(copy(block, m[k], piece, onward))
        along_y[name, k] = go(copy(block, m[k], piece, to_up if k == 0 else to_down))

    def to_the_mate(name, block, row):
        mate[name].append(go(copy(block, row, half, to_mate)))

    def pass_on(name, block):
        for k in range(2):
            along_y[name, k].wait_recv()
        to_the_mate(name, block, o[0])

    def arrived_all(name):
        for c in mate[name]:
            c.wait_recv()

    i_left.wait_recv()
    i_far = send_idx(lb, to_right)
    i_mates = [send_idx(lb, to_mate)]
    i_right.wait_recv()
    i_mates.append(send_idx(rb, to_mate))
    relay("l", lb, 0, from_left[0], to_right)
    relay("r", rb, 1, from_right[1], to_left)
    s_mate.wait_recv()
    for c in small:
        c.wait()
    pair(0, x)
    relay("l", lb, 1, from_left[1])
    relay("r", rb, 0, from_right[0])
    to_the_mate("l", lb, m[0])
    to_the_mate("r", rb, m[0])
    i_far.wait_recv()
    i_mates.append(send_idx(fb, to_mate))
    relay("f", fb, 0, forward[0])
    relay("f", fb, 1, forward[1])
    to_the_mate("f", fb, m[0])
    pass_on("l", lb)
    pass_on("r", rb)
    arrived_all("l")
    pair(1, left)
    pass_on("f", fb)
    arrived_all("r")
    pair(2, right)
    first = pl.multiple_of(own * n_local, n_local)
    lst_rows = 2 * n_x * rows // LANES
    lst_ref[n_local * lst_rows:, :] = jnp.full((lst_ref.shape[0] - n_local * lst_rows, LANES), 2 * n_x * rows, jnp.int32)
    for c in [i_own] + i_mates:
        c.wait_recv()
    routing_lists(jnp.concatenate([idx[b] for b in range(2 * n_x)], axis=1), first, n_local, lst_ref, cnt_ref)
    arrived_all("f")
    pair(3, far)
    n_hi = 2 * n_x * rows // LANES
    wl_ref[...] = jnp.zeros_like(wl_ref)
    for b in range(n_x):
        wt = prob[b, pl.ds(first, n_local), :]
        for e in range(n_local):
            for c in range(2):
                wl_ref[e * (n_hi + 1) + 2 * b + c:e * (n_hi + 1) + 2 * b + c + 1, :] = (
                    wt[e:e + 1, c * LANES:(c + 1) * LANES])
    for c in started + icopies:
        c.wait_send()
    for c in outs:
        c.wait()


def run_gather(hidden, idx_t, gain, rw_t, sig_t, shg_t, shu_t, n_local, n_x):
    rows, dim = hidden.shape
    n_tok = rows * 2 * n_x
    n_hi = n_tok // LANES
    n_exp, width = rw_t.shape[0], shg_t.shape[0]
    pad = (width + 15) // 16 * 16
    n_copy = 4 + 1 + 2 + 6 + 6
    n_idx = 3 + 1 + 3
    vmem = pl.BlockSpec(memory_space=pltpu.VMEM)
    hbm = pl.BlockSpec(memory_space=pl.ANY)
    return pl.pallas_call(
        functools.partial(gather_kernel, n_local),
        out_shape=(jax.ShapeDtypeStruct((n_tok, dim), BF16),
                   jax.ShapeDtypeStruct((width, n_tok), BF16),
                   jax.ShapeDtypeStruct((n_tok, 1), F32),
                   jax.ShapeDtypeStruct(((n_local + 1) * n_hi, LANES), jnp.int32),
                   jax.ShapeDtypeStruct((n_local * (n_hi + 1), LANES), F32),
                   jax.ShapeDtypeStruct((n_local, LANES), jnp.int32)),
        in_specs=[hbm] * 7,
        out_specs=[hbm] + [vmem] * 5,
        scratch_shapes=[
            pltpu.VMEM((2 * n_x, rows, dim), BF16),
            pltpu.VMEM((2 * n_x,) + idx_t.shape, jnp.int32),
            pltpu.VMEM((n_exp + 2 * pad, dim), BF16),
            pltpu.VMEM((dim,), BF16),
            pltpu.VMEM((1, dim), BF16),
            pltpu.VMEM((n_x, n_exp, 2 * rows), F32),
            pltpu.VMEM((n_x, 2 * rows, dim), BF16),
            pltpu.SemaphoreType.DMA((7,)),
            pltpu.SemaphoreType.DMA((n_copy,)),
            pltpu.SemaphoreType.DMA((n_copy,)),
            pltpu.SemaphoreType.DMA((n_idx,)),
            pltpu.SemaphoreType.DMA((n_idx,)),
            pltpu.SemaphoreType.DMA((n_x,)),
        ],
        compiler_params=pltpu.CompilerParams(collective_id=0, has_side_effects=True, vmem_limit_bytes=67_000_000),
        name="gather",
    )(hidden, idx_t, gain, rw_t, sig_t, shg_t, shu_t)


def expert_kernel(lst_hbm, wl_hbm, cnt_hbm, h_hbm, act_hbm, sig_hbm, shd_hbm, wg_hbm, wu_hbm, wd_hbm, out_hbm,
                  lst, wl, cnt, act_ref, sig_ref, shd_ref, h_in, table, acc, wg, wu, wd, xt, xb, fb, active, tile_e, tile_s, tile_r, tile_n,
                  in_sem, w_sem, out_sem, small_sem):
    n_tok, dim = h_hbm.shape
    n_local = wg_hbm.shape[0]
    n_chunk = dim // LANES
    n_blocks = n_tok // LANES
    big = TILES[-1]
    stride = big + PAD

    def fetch_h(b):
        return pltpu.make_async_copy(h_hbm.at[pl.ds(b * LANES, LANES), :], h_in.at[b], in_sem.at[b])

    def weight_copies(e, s):
        return (pltpu.make_async_copy(wg_hbm.at[e], wg.at[s], w_sem.at[s, 0]),
                pltpu.make_async_copy(wu_hbm.at[e], wu.at[s], w_sem.at[s, 1]),
                pltpu.make_async_copy(wd_hbm.at[e], wd.at[s], w_sem.at[s, 2]))

    small = [pltpu.make_async_copy(src, dst, small_sem.at[k]) for k, (src, dst) in enumerate((
        (cnt_hbm, cnt), (lst_hbm, lst), (wl_hbm, wl), (act_hbm, act_ref), (sig_hbm, sig_ref), (shd_hbm, shd_ref)))]
    for c in small:
        c.start()
    for b in range(n_blocks):
        fetch_h(b).start()
    small[0].wait()

    def note(e, carry):
        n, tiles = carry
        total = cnt[e, 0]

        @pl.when(total > 0)
        def _():
            active[n] = e

        def tile(k, t):
            tile_e[t] = e
            tile_s[t] = n
            tile_r[t] = k * big
            tile_n[t] = jnp.minimum(total - k * big, big)
            return t + 1

        return n + jnp.where(total > 0, 1, 0), lax.fori_loop(0, (total + big - 1) // big, tile, tiles)

    n_active, n_tiles = lax.fori_loop(0, n_local, note, (0, 0))
    for s in range(SLOTS - 1):
        @pl.when(s < n_active)
        def _():
            for c in weight_copies(active[s], s):
                c.start()

    acc[n_tok * PITCH:, :] = jnp.zeros((acc.shape[0] - n_tok * PITCH, LANES), F32)
    table[n_tok * PITCH:, :] = jnp.zeros((table.shape[0] - n_tok * PITCH, LANES), F32)

    def shared(b, carry):
        rows = pl.ds(pl.multiple_of(b * LANES, LANES), LANES)
        sig = sig_ref[rows, :]
        for c in range(0, n_chunk, 2):
            sh = sig * lax.dot_general(act_ref[:, rows], shd_ref[:, c * LANES:(c + 2) * LANES], TN,
                                       preferred_element_type=F32)
            for d in range(2):
                acc[pl.ds(b * LANES * PITCH + c + d, LANES, stride=PITCH), :] = sh[:, d * LANES:(d + 1) * LANES]
        return carry

    for c in small[1:]:
        c.wait()
    lax.fori_loop(0, n_blocks, shared, 0)

    def spread(b, carry):
        fetch_h(b).wait()
        for c in range(n_chunk):
            table[pl.ds(b * LANES * PITCH + c, LANES, stride=PITCH), :] = (
                h_in[b, :, c * LANES:(c + 1) * LANES].astype(F32))
        return carry

    lax.fori_loop(0, n_blocks, spread, 0)

    def gather8(base, g):
        for i in range(8):
            row = pl.multiple_of(lst[base + g * 8 + i] * PITCH, 4)
            xt[pl.ds(g * 8 + i, n_chunk, stride=stride), :] = table[pl.ds(row, n_chunk), :]

    def scatter8(f_at, w_at, base, g):
        where, weight, old, new = [], [], [], []
        for i in range(8):
            t = lst[base + g * 8 + i]
            where.append(pl.multiple_of(t * PITCH, 4))
            weight.append(wl[w_at + t])
            old.append(acc[pl.ds(where[i], n_chunk), :])
        for i in range(8):
            new.append(old[i] + weight[i] * fb[pl.ds(f_at + g * 8 + i, n_chunk, stride=stride), :])
        for i in range(8):
            acc[pl.ds(where[i], n_chunk), :] = new[i]

    def ffn(m, s, f_at, moves):
        for c in range(n_chunk):
            xb[:m, c * LANES:(c + 1) * LANES] = xt[c * stride:c * stride + m, :].astype(BF16)
        n_move = len(moves)
        done = 0

        def some(upto):
            nonlocal done
            while done < upto:
                moves[done]()
                done += 1

        gate = lax.dot_general(wg[s], xb[:m, :], NT, preferred_element_type=F32)
        some(n_move * 3 // 10)
        up = lax.dot_general(wu[s], xb[:m, :], NT, preferred_element_type=F32)
        some(n_move * 6 // 10)
        act = (jax.nn.silu(gate) * up).astype(BF16)
        for c in range(0, n_chunk, 2):
            f = lax.dot_general(act, wd[s, :, c * LANES:(c + 2) * LANES], TN, preferred_element_type=F32)
            yield_at = n_move * 6 // 10 + (n_move - n_move * 6 // 10) * (c + 2) // n_chunk
            for d in range(2):
                fb[pl.ds(f_at + (c + d) * stride, m), :] = f[:, d * LANES:(d + 1) * LANES]
            some(yield_at)

    @pl.when(n_tiles > 0)
    def _():
        def first(g, carry):
            gather8(tile_e[0] * n_tok + tile_r[0], g)
            return carry

        lax.fori_loop(0, (tile_n[0] + 7) // 8, first, 0)

    def tile_step(i, carry):
        e, k, r0, n = tile_e[i], tile_s[i], tile_r[i], tile_n[i]
        s = lax.rem(k, SLOTS)

        @pl.when(r0 == 0)
        def _():
            ahead = k + SLOTS - 1

            @pl.when(ahead < n_active)
            def _():
                for c in weight_copies(active[ahead], lax.rem(ahead, SLOTS)):
                    c.start()

            for c in weight_copies(e, s):
                c.wait()

        f_size = n_chunk * stride
        f_at = pl.multiple_of(lax.rem(i, 2) * f_size, 8)
        f_prev = pl.multiple_of(lax.rem(i + 1, 2) * f_size, 8)
        before, after = jnp.maximum(i - 1, 0), jnp.minimum(i + 1, n_tiles - 1)
        e1 = tile_e[before]
        w1 = e1 * (n_tok + LANES)
        base1 = jnp.where(i > 0, e1 * n_tok + tile_r[before], n_local * n_tok)
        n1 = jnp.where(i > 0, tile_n[before], 0)
        base2 = tile_e[after] * n_tok + tile_r[after]
        n2 = jnp.where(i + 1 < n_tiles, tile_n[after], 0)
        below = 0
        for m in TILES:
            @pl.when((n > below) & (n <= m))
            def _(m=m):
                moves = []
                for g in range(m // 8):
                    moves.append(functools.partial(gather8, base2, g))
                    moves.append(functools.partial(scatter8, f_prev, w1, base1, g))
                ffn(m, s, f_at, moves)

                def more_in(g, c2):
                    gather8(base2, g)
                    return c2

                def more_out(g, c2):
                    scatter8(f_prev, w1, base1, g)
                    return c2

                lax.fori_loop(m // 8, (n2 + 7) // 8, more_in, 0)
                lax.fori_loop(m // 8, (n1 + 7) // 8, more_out, 0)
            below = m

        return carry

    lax.fori_loop(0, n_tiles, tile_step, 0)

    @pl.when(n_tiles > 0)
    def _():
        i = n_tiles - 1
        f_at = pl.multiple_of(lax.rem(i, 2) * (n_chunk * stride), 8)

        def last(g, carry):
            scatter8(f_at, tile_e[i] * (n_tok + LANES), tile_e[i] * n_tok + tile_r[i], g)
            return carry

        lax.fori_loop(0, (tile_n[i] + 7) // 8, last, 0)

    def write_out(b):
        return pltpu.make_async_copy(h_in.at[b], out_hbm.at[pl.ds(b * LANES, LANES), :], out_sem.at[b])

    def finish(b, carry):
        for c in range(n_chunk):
            h_in[b, :, c * LANES:(c + 1) * LANES] = (
                acc[pl.ds(b * LANES * PITCH + c, LANES, stride=PITCH), :].astype(BF16))
        write_out(b).start()
        return carry

    lax.fori_loop(0, n_blocks, finish, 0)
    for b in range(n_blocks):
        write_out(b).wait()


def run_experts(lst, wl, cnt, h, act, sig, shd, wg, wu, wd):
    n_tok, dim = h.shape
    n_local, width, _ = wg.shape
    n_chunk = dim // LANES
    big = TILES[-1]
    max_tiles = n_local * ((n_tok + big - 1) // big)
    hbm = pl.BlockSpec(memory_space=pl.ANY)
    return pl.pallas_call(
        expert_kernel,
        out_shape=jax.ShapeDtypeStruct((n_tok, dim), BF16),
        in_specs=[hbm] * 10,
        out_specs=hbm,
        scratch_shapes=[
            pltpu.SMEM((lst.size,), jnp.int32),
            pltpu.SMEM((wl.size,), F32),
            pltpu.SMEM(cnt.shape, jnp.int32),
            pltpu.VMEM(act.shape, BF16),
            pltpu.VMEM(sig.shape, F32),
            pltpu.VMEM(shd.shape, BF16),
            pltpu.VMEM((n_tok // LANES, LANES, dim), BF16),
            pltpu.VMEM(((n_tok + 1) * PITCH, LANES), F32),
            pltpu.VMEM(((n_tok + 1) * PITCH, LANES), F32),
            pltpu.VMEM((SLOTS, width, dim), BF16),
            pltpu.VMEM((SLOTS, width, dim), BF16),
            pltpu.VMEM((SLOTS, width, dim), BF16),
            pltpu.VMEM((n_chunk * (big + PAD), LANES), F32),
            pltpu.VMEM((big, dim), BF16),
            pltpu.VMEM((2 * n_chunk * (big + PAD), LANES), F32),
            pltpu.SMEM((n_local,), jnp.int32),
            pltpu.SMEM((max_tiles,), jnp.int32),
            pltpu.SMEM((max_tiles,), jnp.int32),
            pltpu.SMEM((max_tiles,), jnp.int32),
            pltpu.SMEM((max_tiles,), jnp.int32),
            pltpu.SemaphoreType.DMA((n_tok // LANES,)),
            pltpu.SemaphoreType.DMA((SLOTS, 3)),
            pltpu.SemaphoreType.DMA((n_tok // LANES,)),
            pltpu.SemaphoreType.DMA((6,)),
        ],
        compiler_params=pltpu.CompilerParams(vmem_limit_bytes=67_000_000),
        name="experts",
    )(lst.reshape(-1), wl.reshape(-1), cnt, h, act, sig, shd, wg, wu, wd)


def reduce_kernel(groups, p_hbm, x_hbm, out_ref, x_ref, last, mate, own, ra, rb, rc, sems):
    x, core, y, n_x, n_y = place()
    rows, dim = x_ref.shape
    part = rows // n_y
    load_x = pltpu.make_async_copy(x_hbm, x_ref, sems[-1])
    s_in, s_d, r_d, s_a, r_a, s_b, r_b, s_c, r_c, s_e, r_e = sems[:-1]

    def at(v, n):
        return lax.rem(v + n, n)

    xs = [at(x + d, n_x) for d in range(4)]
    ys = [at(y + d, n_y) for d in range(4)]
    to_mate = peer(x, 1 - core, y)
    x_peers = [None] + [peer(xs[d], core, y) for d in range(1, 4)]
    y_peers = [None] + [peer(x, core, ys[d]) for d in range(1, 4)]
    mine = pl.ds(pl.multiple_of(y * part, part), part)
    started = []

    def go(c):
        c.start()
        started.append(c)
        return c

    loads, mates = [], []
    for g, (kind, lo, w) in enumerate(groups):
        c = pltpu.make_async_copy(p_hbm.at[:, core, :, lo:lo + w], own[g], s_in.at[g])
        c.start()
        loads.append(c)
    load_x.start()
    meet([to_mate] + x_peers[1:] + y_peers[1:])
    for g, (kind, lo, w) in enumerate(groups):
        mates.append(go(remote(p_hbm.at[:, 1 - core, :, lo:lo + w], mate[g], s_d.at[g], r_d.at[g], to_mate)))

    def unit(g, d, lo, n):
        if groups[g][0] == "x":
            return own[g].at[xs[d], lo:lo + n, :]
        return own[g].at[:, pl.ds(pl.multiple_of(ys[d] * part, part) + lo, n), :]

    def land(g, k, lo, n):
        return rb[g].at[k, lo:lo + n, :] if groups[g][0] == "x" else rb[g].at[k, :, lo:lo + n, :]

    def first_peers(g):
        return x_peers if groups[g][0] == "x" else y_peers

    def half(g):
        return (rows if groups[g][0] == "x" else part) // 2

    a, b_ind, b_dep, c_sent, e_sent = {}, {}, {}, {}, {}

    def add_mate(g):
        loads[g].wait()
        mates[g].wait_recv()
        own[g][...] = (own[g][...].astype(F32) + mate[g][...].astype(F32)).astype(BF16)
        h = half(g)
        for k, (lo, d) in enumerate(((0, 1), (h, 3))):
            a[g, k] = go(remote(unit(g, 2, lo, h), ra[g].at[k], s_a.at[g, k], r_a.at[g, k], first_peers(g)[d]))

    def send_near(g):
        h = half(g)
        for k, (lo, d) in enumerate(((h, 1), (0, 3))):
            b_ind[g, k] = go(remote(unit(g, d, lo, h), land(g, k, lo, h), s_b.at[g, k, 0], r_b.at[g, k, 0],
                                    first_peers(g)[d]))

    def add_far(g):
        h = half(g)
        for k, (lo, d) in enumerate(((0, 1), (h, 3))):
            a[g, k].wait_recv()
            ref = unit(g, d, lo, h)
            ref[...] = (ref[...].astype(F32) + ra[g][k].astype(F32)).astype(BF16)
            b_dep[g, k] = go(remote(ref, land(g, k, lo, h), s_b.at[g, k, 1], r_b.at[g, k, 1], first_peers(g)[d]))

    def second_axis(g):
        for k in range(2):
            b_ind[g, k].wait_recv()
            b_dep[g, k].wait_recv()
        ref = unit(g, 0, 0, 2 * half(g))
        ref[...] = (ref[...].astype(F32) + rb[g][0].astype(F32) + rb[g][1].astype(F32)).astype(BF16)
        for d in (2, 1, 3):
            if groups[g][0] == "x":
                src = own[g].at[x, pl.ds(pl.multiple_of(ys[d] * part, part), part), :]
                where = y_peers[d]
            else:
                src = own[g].at[xs[d], mine, :]
                where = x_peers[d]
            c_sent[g, d] = go(remote(src, rc[g].at[d - 1], s_c.at[g, d - 1], r_c.at[g, d - 1], where))

    def finish(g):
        kind, lo, w = groups[g]
        if g == 0:
            load_x.wait()
        total = own[g][x, mine, :].astype(F32)
        for d in (1, 3, 2):
            c_sent[g, d].wait_recv()
            total = total + rc[g][d - 1].astype(F32)
        cols = slice(lo, lo + w)
        out_ref[mine, cols] = (x_ref[mine, cols].astype(F32) + total).astype(BF16)
        for d in (2, 1, 3):
            ref = out_ref.at[mine, cols]
            e_sent[g, d] = go(remote(ref, ref, s_e.at[g, d - 1], r_e.at[g, d - 1], y_peers[d]))

    def exchange(g):
        for k in range(2):
            b_ind[g, k].wait_recv()
            b_dep[g, k].wait_recv()
        last[y] = (own[g][x].astype(F32) + rb[g][0].astype(F32) + rb[g][1].astype(F32)).astype(BF16)
        for d in (2, 1, 3):
            c_sent[g, d] = go(remote(last.at[y], last.at[y], s_c.at[g, d - 1], r_c.at[g, d - 1], y_peers[d]))

    def close(g):
        _, lo, w = groups[g]
        for d in (1, 3, 2):
            c_sent[g, d].wait_recv()
        total = last[0].astype(F32)
        for k in range(1, 4):
            total = total + last[k].astype(F32)
        out_ref[:, lo:lo + w] = (x_ref[:, lo:lo + w].astype(F32) + total).astype(BF16)

    order = ((add_mate, 0), (send_near, 0), (add_mate, 1), (send_near, 1), (add_mate, 2), (send_near, 2), (add_far, 0),
             (add_far, 1), (add_mate, 3), (add_far, 2), (second_axis, 0), (send_near, 3), (second_axis, 2),
             (add_mate, 4), (second_axis, 1), (add_far, 3), (send_near, 4), (finish, 0), (finish, 2), (add_far, 4),
             (finish, 1), (second_axis, 3), (exchange, 4), (finish, 3), (close, 4))
    for step, g in order:
        step(g)
    for g in range(len(groups) - 1):
        for d in range(1, 4):
            e_sent[g, d].wait_recv()
    for c in started:
        c.wait_send()


def run_reduce(partial, hidden, n_x, n_y):
    rows, dim = hidden.shape
    q = dim // 8
    groups = (("x", 0, q), ("x", q, 2 * q), ("y", 3 * q, 2 * q), ("x", 5 * q, 2 * q), ("x", 7 * q, q))
    n_g = len(groups)
    part = rows // n_y
    dma = pltpu.SemaphoreType.DMA

    def per_group(of):
        return [pltpu.VMEM(of(kind, w), BF16) for kind, _, w in groups]

    def kernel(p, xh, o, xr, last, *rest):
        lists = [rest[k * n_g:(k + 1) * n_g] for k in range(5)]
        reduce_kernel(groups, p, xh, o, xr, last, *lists, rest[5 * n_g:])

    return pl.pallas_call(
        kernel,
        out_shape=jax.ShapeDtypeStruct((rows, dim), BF16),
        in_specs=[pl.BlockSpec(memory_space=pltpu.HBM)] * 2,
        out_specs=pl.BlockSpec(memory_space=pltpu.VMEM),
        scratch_shapes=(
            [pltpu.VMEM((rows, dim), BF16), pltpu.VMEM((n_y, rows, groups[-1][2]), BF16)] +
            per_group(lambda kind, w: (n_x, rows, w)) + per_group(lambda kind, w: (n_x, rows, w))
            + per_group(lambda kind, w: (2, rows // 2, w) if kind == "x" else (2, n_x, part // 2, w))
            + per_group(lambda kind, w: (2, rows, w) if kind == "x" else (2, n_x, part, w))
            + per_group(lambda kind, w: (3, part, w))
            + [dma((n_g,)), dma((n_g,)), dma((n_g,)), dma((n_g, 2)), dma((n_g, 2)), dma((n_g, 2, 2)),
               dma((n_g, 2, 2)), dma((n_g, 3)), dma((n_g, 3)), dma((n_g, 3)), dma((n_g, 3)), dma]),
        compiler_params=pltpu.CompilerParams(collective_id=1, has_side_effects=True, vmem_limit_bytes=60_000_000),
        name="reduce",
    )(partial.reshape(n_x, 2, rows, dim), hidden)


def solution(mesh):
    tok_spec = P(('dp', 'ep'), None)
    in_specs = (tok_spec, tok_spec, P(None), P(None, None), P(None, None),
                P('ep', None, 'tp'), P('ep', None, 'tp'), P('ep', 'tp', None),
                P(None, ('tp', 'ep')), P(None, ('tp', 'ep')), P(('tp', 'ep'), None))
    n_x, n_y = mesh.shape['ep'] // 2, mesh.shape['tp']
    assert n_x == 4 and n_y == 4

    def local_step(hidden_in, topk_idx, norm_gain, router_w, shared_sig_w, exp_gate, exp_up, exp_down,
                   sh_gate, sh_up, sh_down):
        h, act, sig, lst, wl, cnt = run_gather(
            hidden_in, topk_idx.T, norm_gain, router_w.T, shared_sig_w.T, sh_gate.T, sh_up.T,
            exp_gate.shape[0], n_x)
        partial = run_experts(lst, wl, cnt, h, act, sig, sh_down,
                              jnp.swapaxes(exp_gate, 1, 2), jnp.swapaxes(exp_up, 1, 2), exp_down)
        return run_reduce(partial, hidden_in, n_x, n_y)

    return jax.shard_map(local_step, mesh=mesh, in_specs=in_specs, out_specs=tok_spec, check_vma=False)
```

profile of v0, /device:TPU:96, one launch (start us, length us, event | category | flops | bytes accessed | tf_op | source)
XLA Modules:
  0.0 87.1 jit_solution(4464744816583687750)
XLA Ops:
  0.0 26.7 %gather.1 = (bf16[1024,2048]{1,0:T(8,128)(2,1)}, bf16[88,1024]{1,0:T(8,128)(2,1)}, f32[1024,1]{1,0:T(8,128)}, s32[72,128]{1,0:T(8,128)}, f32[72,128]{1,0:T(8,128)}, /*index=5*/s32[8,128]{1,0:T(8,128)}) custom-call(bf16[128,2048]{1,0:T(8,128)(2,1)} %xh.1, s32[6,128]{1,0:T(8,128)} %bitcast.19, bf16[2048]{0:T(1024)(128)(2,1)} %gain_hbm.1, ...), custom_call_target="tpu_custom_call" | custom-call | tf_op jit(solution)/shard_map/gather/pallas_call | solution.py:262
  26.7 20.3 %experts.1 = bf16[1024,2048]{1,0:T(8,128)(2,1)} custom-call(s32[9216]{0:T(1024)} %bitcast.16, f32[9216]{0:T(1024)} %bitcast.17, s32[8,128]{1,0:T(8,128)} %get-tuple-element.13.cnt_hbm, bf16[1024,2048]{1,0:T(8,128)(2,1)} %get-tuple-element.14.h_hbm, bf16[88,1024]{1,0:T(8,128)(2,1)} %get-tuple-element.15.act_hbm, f32[1024,1]{1,0:T(8,128)} %get-tuple-element.16.sig_hbm, ...), custom_call_target="tpu_custom_call" | custom-call | tf_op jit(solution)/shard_map/experts/pallas_call | solution.py:502
  47.0 38.2 %reduce.1 = bf16[128,2048]{1,0:T(8,128)(2,1)} custom-call(bf16[4,2,128,2048]{3,2,1,0:T(8,128)(2,1)} %bitcast.10, bf16[128,2048]{1,0:T(8,128)(2,1)} %xh.1), custom_call_target="tpu_custom_call" | custom-call | tf_op jit(solution)/shard_map/reduce/pallas_call | solution.py:683
  85.2 1.9 %copy.13 = bf16[128,2048]{1,0:T(8,128)(2,1)} copy(bf16[128,2048]{1,0:T(8,128)(2,1)} %reduce.1) | data formatting | bytes 1048576
where the time goes:
time: 87 us; the launch traced here: 87.1 us
  Pallas kernels  85.2 us (98%)
  local copies, waits for them, and re-layouts  1.88 us (2%)
    pallas_call x1, Pallas kernels, run_reduce(): pl.pallas_call(kernel, out_shape=jax.ShapeDtypeStruct((rows, dim), BF16),...  38.2 us
    pallas_call x1, Pallas kernels, run_gather(): pl.pallas_call(functools.partial(gather_kernel, n_local), out_shape=(jax....  26.7 us
    pallas_call x1, Pallas kernels, run_experts(): pl.pallas_call(expert_kernel, out_shape=jax.ShapeDtypeStruct((n_tok, dim)...  20.3 us
    unnamed x1, local copies, waits for them, and re-layouts  1.88 us

commit v1 on v0

--- a/solution.py
+++ b/solution.py
@@ -652,10 +652,9 @@
             total = total + last[k].astype(F32)
         out_ref[:, lo:lo + w] = (x_ref[:, lo:lo + w].astype(F32) + total).astype(BF16)
 
-    order = ((add_mate, 0), (send_near, 0), (add_mate, 1), (send_near, 1), (add_mate, 2), (send_near, 2), (add_far, 0),
-             (add_far, 1), (add_mate, 3), (add_far, 2), (second_axis, 0), (send_near, 3), (second_axis, 2),
-             (add_mate, 4), (second_axis, 1), (add_far, 3), (send_near, 4), (finish, 0), (finish, 2), (add_far, 4),
-             (finish, 1), (second_axis, 3), (exchange, 4), (finish, 3), (close, 4))
+    order = ((add_mate, 0), (send_near, 0), (add_mate, 1), (send_near, 1), (add_mate, 2), (add_far, 0), (send_near, 2),
+             (add_far, 1), (add_mate, 3), (add_far, 2), (second_axis, 0), (second_axis, 1), (send_near, 3),
+             (add_far, 3), (finish, 0), (second_axis, 2), (finish, 1), (exchange, 3), (finish, 2), (close, 3))
     for step, g in order:
         step(g)
     for g in range(len(groups) - 1):
@@ -668,7 +667,7 @@
 def run_reduce(partial, hidden, n_x, n_y):
     rows, dim = hidden.shape
     q = dim // 8
-    groups = (("x", 0, q), ("x", q, 2 * q), ("y", 3 * q, 2 * q), ("x", 5 * q, 2 * q), ("x", 7 * q, q))
+    groups = (("x", 0, 2 * q), ("y", 2 * q, 2 * q), ("x", 4 * q, 3 * q), ("x", 7 * q, q))
     n_g = len(groups)
     part = rows // n_y
     dma = pltpu.SemaphoreType.DMA
@@ -693,7 +692,7 @@
             + per_group(lambda kind, w: (3, part, w))
             + [dma((n_g,)), dma((n_g,)), dma((n_g,)), dma((n_g, 2)), dma((n_g, 2)), dma((n_g, 2, 2)),
                dma((n_g, 2, 2)), dma((n_g, 3)), dma((n_g, 3)), dma((n_g, 3)), dma((n_g, 3)), dma]),
-        compiler_params=pltpu.CompilerParams(collective_id=1, has_side_effects=True, vmem_limit_bytes=60_000_000),
+        compiler_params=pltpu.CompilerParams(collective_id=1, has_side_effects=True, vmem_limit_bytes=56_000_000),
         name="reduce",
     )(partial.reshape(n_x, 2, rows, dim), hidden)
 

time: 87 us -> 83.9 us (0.964)
  the two profiles are of different devices: /device:TPU:96 before, /device:TPU:97 now
where the time goes in v1:
time: 83.9 us; the launch traced here: 83.5 us
  Pallas kernels  82.6 us (98%)
    pallas_call x1, Pallas kernels, run_reduce(): pl.pallas_call(kernel, out_shape=jax.ShapeDtypeStruct((rows, dim), BF16),...  37.7 us
    pallas_call x1, Pallas kernels, run_gather(): pl.pallas_call(functools.partial(gather_kernel, n_local), out_shape=(jax....  28.1 us
    pallas_call x1, Pallas kernels, run_experts(): pl.pallas_call(expert_kernel, out_shape=jax.ShapeDtypeStruct((n_tok, dim)...  16.9 us

profile of v1, /device:TPU:97, one launch (start us, length us, event | category | flops | bytes accessed | tf_op | source)
XLA Modules:
  0.0 83.5 jit_solution(18313013055354826324)
XLA Ops:
  0.0 28.1 %gather.1 = (bf16[1024,2048]{1,0:T(8,128)(2,1)}, bf16[88,1024]{1,0:T(8,128)(2,1)}, f32[1024,1]{1,0:T(8,128)}, s32[72,128]{1,0:T(8,128)}, f32[72,128]{1,0:T(8,128)}, /*index=5*/s32[8,128]{1,0:T(8,128)}) custom-call(bf16[128,2048]{1,0:T(8,128)(2,1)} %xh.1, s32[6,128]{1,0:T(8,128)} %bitcast.19, bf16[2048]{0:T(1024)(128)(2,1)} %gain_hbm.1, ...), custom_call_target="tpu_custom_call" | custom-call | tf_op jit(solution)/shard_map/gather/pallas_call | solution.py:262
  28.1 16.9 %experts.1 = bf16[1024,2048]{1,0:T(8,128)(2,1)} custom-call(s32[9216]{0:T(1024)} %bitcast.16, f32[9216]{0:T(1024)} %bitcast.17, s32[8,128]{1,0:T(8,128)} %get-tuple-element.13.cnt_hbm, bf16[1024,2048]{1,0:T(8,128)(2,1)} %get-tuple-element.14.h_hbm, bf16[88,1024]{1,0:T(8,128)(2,1)} %get-tuple-element.15.act_hbm, f32[1024,1]{1,0:T(8,128)} %get-tuple-element.16.sig_hbm, ...), custom_call_target="tpu_custom_call" | custom-call | tf_op jit(solution)/shard_map/experts/pallas_call | solution.py:502
  45.0 37.7 %reduce.1 = bf16[128,2048]{1,0:T(8,128)(2,1)S(1)} custom-call(bf16[4,2,128,2048]{3,2,1,0:T(8,128)(2,1)} %bitcast.10, bf16[128,2048]{1,0:T(8,128)(2,1)} %xh.1), custom_call_target="tpu_custom_call" | custom-call | tf_op jit(solution)/shard_map/reduce/pallas_call | solution.py:682
  82.7 0.8 copy.13

commit v2 on v1

--- a/solution.py
+++ b/solution.py
@@ -224,15 +224,15 @@
     pass_on("r", rb)
     arrived_all("l")
     pair(1, left)
-    pass_on("f", fb)
-    arrived_all("r")
-    pair(2, right)
     first = pl.multiple_of(own * n_local, n_local)
     lst_rows = 2 * n_x * rows // LANES
     lst_ref[n_local * lst_rows:, :] = jnp.full((lst_ref.shape[0] - n_local * lst_rows, LANES), 2 * n_x * rows, jnp.int32)
     for c in [i_own] + i_mates:
         c.wait_recv()
     routing_lists(jnp.concatenate([idx[b] for b in range(2 * n_x)], axis=1), first, n_local, lst_ref, cnt_ref)
+    pass_on("f", fb)
+    arrived_all("r")
+    pair(2, right)
     arrived_all("f")
     pair(3, far)
     n_hi = 2 * n_x * rows // LANES

time: 83.9 us -> 84.2 us (level)
  the two profiles are of different devices: /device:TPU:97 before, /device:TPU:96 now
where the time goes in v2:
time: 84.2 us; the launch traced here: 83.1 us
  Pallas kernels  82.3 us (98%)
    pallas_call x1, Pallas kernels, run_reduce(): pl.pallas_call(kernel, out_shape=jax.ShapeDtypeStruct((rows, dim), BF16),...  34.4 us
    pallas_call x1, Pallas kernels, run_gather(): pl.pallas_call(functools.partial(gather_kernel, n_local), out_shape=(jax....  26.1 us
    pallas_call x1, Pallas kernels, run_experts(): pl.pallas_call(expert_kernel, out_shape=jax.ShapeDtypeStruct((n_tok, dim)...  21.8 us

profile of v2, /device:TPU:96, one launch (start us, length us, event | category | flops | bytes accessed | tf_op | source)
XLA Modules:
  0.0 83.1 jit_solution(6517554341729782373)
XLA Ops:
  0.0 26.1 %gather.1 = (bf16[1024,2048]{1,0:T(8,128)(2,1)}, bf16[88,1024]{1,0:T(8,128)(2,1)}, f32[1024,1]{1,0:T(8,128)}, s32[72,128]{1,0:T(8,128)}, f32[72,128]{1,0:T(8,128)}, /*index=5*/s32[8,128]{1,0:T(8,128)}) custom-call(bf16[128,2048]{1,0:T(8,128)(2,1)} %xh.1, s32[6,128]{1,0:T(8,128)} %bitcast.19, bf16[2048]{0:T(1024)(128)(2,1)} %gain_hbm.1, ...), custom_call_target="tpu_custom_call" | custom-call | tf_op jit(solution)/shard_map/gather/pallas_call | solution.py:262
  26.1 21.8 %experts.1 = bf16[1024,2048]{1,0:T(8,128)(2,1)} custom-call(s32[9216]{0:T(1024)} %bitcast.16, f32[9216]{0:T(1024)} %bitcast.17, s32[8,128]{1,0:T(8,128)} %get-tuple-element.13.cnt_hbm, bf16[1024,2048]{1,0:T(8,128)(2,1)} %get-tuple-element.14.h_hbm, bf16[88,1024]{1,0:T(8,128)(2,1)} %get-tuple-element.15.act_hbm, f32[1024,1]{1,0:T(8,128)} %get-tuple-element.16.sig_hbm, ...), custom_call_target="tpu_custom_call" | custom-call | tf_op jit(solution)/shard_map/experts/pallas_call | solution.py:502
  47.9 34.4 %reduce.1 = bf16[128,2048]{1,0:T(8,128)(2,1)S(1)} custom-call(bf16[4,2,128,2048]{3,2,1,0:T(8,128)(2,1)} %bitcast.10, bf16[128,2048]{1,0:T(8,128)(2,1)} %xh.1), custom_call_target="tpu_custom_call" | custom-call | tf_op jit(solution)/shard_map/reduce/pallas_call | solution.py:682
  82.3 0.8 copy.13
